TPU v7x, 256 devices: a whole 4x4x8 slice. The times are simulated.
256 devices in a mesh: leaf: 64 (over z, y, core), front: 4 (over x).
Axes of the slice: x: 4, y: 4, z: 8, core: 2. Of those that a mesh axis runs over, the one named last changes fastest.
Arguments:
- rhs_leaf: float32 [32, 65536], P(None, ('leaf', 'front')), may hold values from -6 to 6
- rhs_sep: float32 [32, 32768], P(None, ('leaf', 'front')), may hold values from -6 to 6
- inv_leaf: float32 [64, 1024, 1024], P('leaf', 'front'), may hold values from -0.1875 to 0.1875
- inv_sep: float32 [64, 512, 512], P('leaf', 'front'), may hold values from -0.25 to 0.25
- push_leaf: float32 [64, 128, 1024], P('leaf', None, 'front'), may hold values from -0.09375 to 0.09375
- push_sep: float32 [64, 128, 512], P('leaf', None, 'front'), may hold values from -0.125 to 0.125
- pull_leaf: float32 [64, 1024, 128], P('leaf', 'front'), may hold values from -0.25 to 0.25
- pull_sep: float32 [64, 512, 128], P('leaf', 'front'), may hold values from -0.25 to 0.25
- rows_leaf: int32 [64, 128], P('leaf'), may hold values from 0 to 511, as said below
- rows_sep: int32 [64, 128], P('leaf'), may hold values from 0 to 511, as said below
- pivot_leaf: int32 [64, 1024], P('leaf'), may hold values from 0 to 1023, each once within a row
- pivot_sep: int32 [64, 512], P('leaf'), may hold values from 0 to 511, each once within a row
- basis_leaf: float32 [50, 65536], P(None, ('leaf', 'front')), may hold values from -6 to 6
- basis_sep: float32 [50, 32768], P(None, ('leaf', 'front')), may hold values from -6 to 6
Outputs:
- q_leaf: float32 [32, 65536], P(None, ('leaf', 'front'))
- q_sep: float32 [32, 32768], P(None, ('leaf', 'front'))
- coeffs: float32 [50, 32], replicated
- rfac: float32 [32, 32], replicated
Inputs may be any that keep to these rules, and one draw needn't show every extreme that they name: `rows_leaf`: each row holds 128 different rows of a separator front. `rows_sep`: each row holds 128 different rows of a separator front. `pivot_leaf`: each row is a permutation. `pivot_sep`: each row is a permutation.
All inputs are finite; a program needn't handle non-finite values.
Results may differ from a plain program's by a relative error of at most 0.0001.
Values sent between devices are 32-bit elements; how exact they have to be, the bound alone decides.
A program may use at most 64 MiB of HBM per device.

v0:
```python
import functools
import jax
import jax.numpy as jnp
from jax import lax
from jax.sharding import Mesh
from jax.sharding import PartitionSpec as P

LEAF = ("leaf_0", "leaf_1", "leaf_2")
LEAF_FRONT = ("leaf_0", "leaf_1", "leaf_2", "front")
exact_mode = lax.Precision.HIGHEST


def cut_along(array, dim, length):
    lengths = array.shape
    pieces = array.reshape(*lengths[:dim], length, lengths[dim] // length, *lengths[dim + 1 :])
    return jnp.moveaxis(pieces, dim, 0)


def sum_at_owner(array, axis, dim):
    pieces = cut_along(array, dim, lax.axis_size(axis))
    arrived = lax.all_to_all(pieces, axis, split_axis=0, concat_axis=0, tiled=True)
    return arrived.sum(axis=0)


def joined_along(pieces, dim):
    pieces = jnp.moveaxis(pieces, 0, dim)
    lengths = pieces.shape
    return pieces.reshape(*lengths[:dim], lengths[dim] * lengths[dim + 1], *lengths[dim + 2 :])


def from_everyone(array, axis):
    copies = jnp.broadcast_to(array, (lax.axis_size(axis), *array.shape))
    return lax.all_to_all(copies, axis, split_axis=0, concat_axis=0, tiled=True)


def gathered_copies(array, axis, dim):
    return joined_along(from_everyone(array, axis), dim)


def rows_first(arrays, axis, dims):
    turned = [jnp.moveaxis(a, dim, 0) for a, dim in zip(arrays, dims)]
    widths = [t[0].size for t in turned]
    both = jnp.concatenate([t.reshape(-1, w) for t, w in zip(turned, widths)], axis=1)
    whole = lax.all_gather(both, axis, axis=0, tiled=True)
    pieces = jnp.split(whole, [sum(widths[:k]) for k in range(1, len(widths))], axis=1)
    return tuple(
        (
            jnp.moveaxis(b.reshape(-1, *t.shape[1:]), 0, dim)
            for b, t, dim in zip(pieces, turned, dims)
        )
    )


def by_axis(array, axes):
    return functools.reduce(lax.psum, axes, array)


def contract(former, latter):
    return lax.dot_general(
        former,
        latter,
        (((1,), (1,)), ((), ())),
        precision=exact_mode,
        preferred_element_type=jnp.float32,
    )


def expand(coeff_block, basis):
    return jnp.dot(coeff_block.T, basis, precision=exact_mode, preferred_element_type=jnp.float32)


def apply_inverse(gathered, inverse, pivots):
    return contract(gathered[:, pivots], inverse)


def solve_if(active, gathered, inverse, pivots):

    def chosen(operand):
        return apply_inverse(operand, inverse, pivots)

    def skipped(operand):
        return jnp.zeros((operand.shape[0], inverse.shape[0]), jnp.float32)

    return lax.cond(active, chosen, skipped, gathered)


def pick_piece(pool, index, valid):
    safe = jnp.clip(index, 0, pool.shape[0] - 1)
    piece = lax.dynamic_index_in_dim(pool, safe, 0, keepdims=False)
    return jnp.where(valid, piece, jnp.zeros_like(piece))


def push_compact(state, weights):
    return sum_at_owner(contract(state, weights), "front", 1)


def sep_gathered(shares):
    return gathered_copies(shares, "front", 1)


def leaf_gathered(shares):
    return gathered_copies(shares, "front", 1)


def on_device(
    rhs_leaf,
    rhs_sep,
    inv_leaf,
    inv_sep,
    push_leaf,
    push_sep,
    pull_leaf,
    pull_sep,
    rows_leaf,
    rows_sep,
    pivot_leaf,
    pivot_sep,
    basis_leaf,
    basis_sep,
):
    holder = lax.axis_index(LEAF)
    groups = lax.axis_size(LEAF)
    top_level = groups.bit_length() - 1
    sep_width = pivot_sep.shape[1]
    share_width = rhs_sep.shape[1]
    leaf_inverse = inv_leaf[0]
    sep_inverse = inv_sep[0]
    leaf_pivots = pivot_leaf[0]
    sep_pivots = pivot_sep[0]
    level_of = jnp.full((), top_level + 1, jnp.int32)
    for bit_index in range(top_level, 0, -1):
        level_of = jnp.where(holder % 2**bit_index != 0, jnp.int32(bit_index), level_of)
    leaf_state = apply_inverse(leaf_gathered(rhs_leaf), leaf_inverse, leaf_pivots)
    sep_state = jnp.zeros_like(rhs_sep)
    leaf_compact = push_compact(leaf_state, push_leaf[0])
    sep_compact = jnp.zeros_like(leaf_compact)
    front_start = lax.axis_index("front") * share_width
    for height in range(1, top_level + 2):
        if height == 1:
            lower_index = holder - 1
            upper_index = holder
        else:
            lower_index = holder - 2 ** (height - 2)
            upper_index = holder + 2 ** (height - 2)
        lower_valid = jnp.logical_and(lower_index >= 0, height <= top_level)
        upper_valid = upper_index < groups
        source = leaf_compact if height == 1 else sep_compact
        source_rows = rows_leaf[0] if height == 1 else rows_sep[0]
        pool, pool_rows = (
            gathered_copies(source[None], LEAF, 0),
            gathered_copies(source_rows[None], LEAF, 0),
        )
        first_part = pick_piece(pool, upper_index, upper_valid)
        first_rows = pick_piece(pool_rows, upper_index, upper_valid)
        second_part = pick_piece(pool, lower_index, lower_valid)
        second_rows = pick_piece(pool_rows, lower_index, lower_valid)
        first_full, second_full = rows_first((first_part, second_part), "front", (1, 1))
        dense = jnp.zeros((rhs_sep.shape[0], sep_width), jnp.float32)
        dense = dense.at[:, first_rows].add(first_full).at[:, second_rows].add(second_full)
        arriving = lax.dynamic_slice_in_dim(dense, front_start, share_width, 1)
        active = level_of == height
        applied = solve_if(active, sep_gathered(rhs_sep - arriving), sep_inverse, sep_pivots)
        sep_state = jnp.where(active, applied, sep_state)
        if height <= top_level:
            sep_compact = jnp.where(active, push_compact(sep_state, push_sep[0]), sep_compact)
    sep_solution = sep_state
    leaf_solution = leaf_state
    for height in range(top_level, -1, -1):
        if height == top_level:
            parent_index = jnp.zeros((), jnp.int32)
        elif height >= 1:
            parent_index = (2 * (holder // 2 ** (height + 1)) + 1) * 2**height
        else:
            parent_index = holder // 2 * 2 + 1
        pool = gathered_copies(sep_solution[None], LEAF, 0)
        picked = lax.dynamic_index_in_dim(pool, parent_index, 0, keepdims=False)
        parent = gathered_copies(picked, "front", 1)
        if height >= 1:
            lifted = contract(parent[:, rows_sep[0]], pull_sep[0])
            active = level_of == height
            applied = solve_if(active, sep_gathered(lifted), sep_inverse, sep_pivots)
            sep_solution = jnp.where(active, sep_state - applied, sep_solution)
        else:
            lifted = contract(parent[:, rows_leaf[0]], pull_leaf[0])
            leaf_solution = leaf_state - apply_inverse(
                leaf_gathered(lifted), leaf_inverse, leaf_pivots
            )
    total_rows = groups * (pivot_leaf.shape[1] + sep_width)
    first_sum, metric_sum = (
        by_axis(
            contract(basis_leaf, leaf_solution) + contract(basis_sep, sep_solution), LEAF_FRONT
        ),
        by_axis(contract(basis_leaf, basis_leaf) + contract(basis_sep, basis_sep), LEAF_FRONT),
    )
    first_proj = first_sum / total_rows
    metric = metric_sum / total_rows
    once_leaf = leaf_solution - expand(first_proj, basis_leaf)
    once_sep = sep_solution - expand(first_proj, basis_sep)
    second_sum, self_sum = (
        by_axis(contract(basis_leaf, once_leaf) + contract(basis_sep, once_sep), LEAF_FRONT),
        by_axis(contract(once_leaf, once_leaf) + contract(once_sep, once_sep), LEAF_FRONT),
    )
    second = second_sum / total_rows
    twice_leaf = once_leaf - expand(second, basis_leaf)
    twice_sep = once_sep - expand(second, basis_sep)
    cross = jnp.dot(second.T, second, precision=exact_mode, preferred_element_type=jnp.float32)
    curved = jnp.dot(
        second.T,
        jnp.dot(metric, second, precision=exact_mode, preferred_element_type=jnp.float32),
        precision=exact_mode,
        preferred_element_type=jnp.float32,
    )
    gram_matrix = self_sum / total_rows - 2.0 * cross + curved
    lower_factor = jnp.linalg.cholesky(gram_matrix)
    q_leaf = lax.linalg.triangular_solve(lower_factor, twice_leaf, left_side=True, lower=True)
    q_sep = lax.linalg.triangular_solve(lower_factor, twice_sep, left_side=True, lower=True)
    return (q_leaf, q_sep, first_proj + second, lower_factor.T)


def solution(mesh):
    torus = Mesh(
        mesh.devices.reshape(8, 4, 2, mesh.shape["front"]), ("leaf_0", "leaf_1", "leaf_2", "front")
    )
    return jax.shard_map(
        on_device,
        mesh=torus,
        in_specs=(
            P(None, LEAF_FRONT),
            P(None, LEAF_FRONT),
            P(LEAF, "front", None),
            P(LEAF, "front", None),
            P(LEAF, None, "front"),
            P(LEAF, None, "front"),
            P(LEAF, "front", None),
            P(LEAF, "front", None),
            P(LEAF, None),
            P(LEAF, None),
            P(LEAF, None),
            P(LEAF, None),
            P(None, LEAF_FRONT),
            P(None, LEAF_FRONT),
        ),
        out_specs=(P(None, LEAF_FRONT), P(None, LEAF_FRONT), P(), P()),
        check_vma=False,
    )
```

profile of v0, /device:TPU:8, one launch (start us, length us, event | category | flops | bytes accessed | tf_op | source)
XLA Modules:
  0.0 963.4 jit_solution(1290878768696683510)
XLA Ops:
  6.6 6.0 all-to-all-done
  17.1 7.7 all_to_all.230
  26.1 12.1 %all-to-all-start.2 = ((s32[64,1,128]{2,1,0:T(1,128)}), s32[64,1,128]{2,1,0:T(1,128)S(1)}, u32[]{:S(2)}, u32[]{:S(2)}) async-start(s32[64,1,128]{2,1,0:T(1,128)} %broadcast_in_dim.199), calls=%async_computation.2 | async-start | bytes 65536 | tf_op jit(solution)/shard_map/all_to_all | solution.py:33
  52.3 12.3 %all-to-all-done.4 = f32[64,1,1024]{2,1,0:T(1,128)S(1)} async-done(((f32[64,1,1024]{2,1,0:T(1,128)}), f32[64,1,1024]{2,1,0:T(1,128)S(1)}, u32[]{:S(2)}, u32[]{:S(2)}) %all-to-all-start.4) | async-done | bytes 262176 | tf_op jit(solution)/shard_map/all_to_all | solution.py:33
  66.3 11.9 %all_gather.21 = f32[128,64]{1,0:T(8,128)S(1)} all-gather(f32[32,64]{1,0:T(8,128)S(1)} %pad_maximum_fusion), channel_id=1, replica_groups=mesh['leaf_0'=8,'leaf_1'=4,'leaf_2'=2,'front'=4] {'front'}, dimensions={0}, use_global_device_ids=true | all-gather | bytes 40960 | tf_op jit(solution)/shard_map/all_gather | solution.py:44
  92.9 7.7 all_to_all.231
  109.8 6.4 all-to-all-done.1
  121.8 12.2 %all-to-all-done.7 = f32[64,1,1024]{2,1,0:T(1,128)S(1)} async-done(((f32[64,1,1024]{2,1,0:T(1,128)}), f32[64,1,1024]{2,1,0:T(1,128)S(1)}, u32[]{:S(2)}, u32[]{:S(2)}) %all-to-all-start.7) | async-done | bytes 262176 | tf_op jit(solution)/shard_map/all_to_all | solution.py:33
  135.7 12.1 %all_gather.22 = f32[128,64]{1,0:T(8,128)S(1)} all-gather(f32[32,64]{1,0:T(8,128)S(1)} %pad_maximum_fusion.1), channel_id=1, replica_groups=mesh['leaf_0'=8,'leaf_1'=4,'leaf_2'=2,'front'=4] {'front'}, dimensions={0}, use_global_device_ids=true | all-gather | bytes 40960 | tf_op jit(solution)/shard_map/all_gather | solution.py:44
  162.2 7.7 all_to_all.232
  171.4 17.6 %all_to_all.233 = f32[64,1,1024]{2,1,0:T(1,128)S(1)} all-to-all(f32[64,1,1024]{2,1,0:T(1,128)S(1)} %reshape.976), channel_id=1, replica_groups=mesh['leaf_0'=8,'leaf_1'=4,'leaf_2'=2,'front'=4] {'leaf_0','leaf_1','lea..., dimensions={0} | all-to-all | bytes 524288 | tf_op jit(solution)/shard_map/all_to_all | solution.py:33
  190.7 11.9 %all_gather.23 = f32[128,64]{1,0:T(8,128)S(1)} all-gather(f32[32,64]{1,0:T(8,128)S(1)} %pad_maximum_fusion.2), channel_id=1, replica_groups=mesh['leaf_0'=8,'leaf_1'=4,'leaf_2'=2,'front'=4] {'front'}, dimensions={0}, use_global_device_ids=true | all-gather | bytes 40960 | tf_op jit(solution)/shard_map/all_gather | solution.py:44
  215.3 7.7 all_to_all.234
  224.5 19.4 %all_to_all.235 = f32[64,1,1024]{2,1,0:T(1,128)S(1)} all-to-all(f32[64,1,1024]{2,1,0:T(1,128)S(1)} %reshape.980), channel_id=1, replica_groups=mesh['leaf_0'=8,'leaf_1'=4,'leaf_2'=2,'front'=4] {'leaf_0','leaf_1','lea..., dimensions={0} | all-to-all | bytes 524288 | tf_op jit(solution)/shard_map/all_to_all | solution.py:33
  245.6 11.9 %all_gather.24 = f32[128,64]{1,0:T(8,128)S(1)} all-gather(f32[32,64]{1,0:T(8,128)S(1)} %pad_maximum_fusion.3), channel_id=1, replica_groups=mesh['leaf_0'=8,'leaf_1'=4,'leaf_2'=2,'front'=4] {'front'}, dimensions={0}, use_global_device_ids=true | all-gather | bytes 40960 | tf_op jit(solution)/shard_map/all_gather | solution.py:44
  270.7 7.7 all_to_all.236
  280.6 6.6 all-to-all-start.16
  287.3 12.2 %all-to-all-done.16 = f32[64,1,1024]{2,1,0:T(1,128)S(1)} async-done(((f32[64,1,1024]{2,1,0:T(1,128)}), f32[64,1,1024]{2,1,0:T(1,128)S(1)}, u32[]{:S(2)}, u32[]{:S(2)}) %all-to-all-start.16) | async-done | bytes 262176 | tf_op jit(solution)/shard_map/all_to_all | solution.py:33
  301.1 11.9 %all_gather.25 = f32[128,64]{1,0:T(8,128)S(1)} all-gather(f32[32,64]{1,0:T(8,128)S(1)} %pad_maximum_fusion.4), channel_id=1, replica_groups=mesh['leaf_0'=8,'leaf_1'=4,'leaf_2'=2,'front'=4] {'front'}, dimensions={0}, use_global_device_ids=true | all-gather | bytes 40960 | tf_op jit(solution)/shard_map/all_gather | solution.py:44
  325.9 7.7 all_to_all.237
  335.1 18.4 %all_to_all.238 = f32[64,1,1024]{2,1,0:T(1,128)S(1)} all-to-all(f32[64,1,1024]{2,1,0:T(1,128)S(1)} %reshape.988), channel_id=1, replica_groups=mesh['leaf_0'=8,'leaf_1'=4,'leaf_2'=2,'front'=4] {'leaf_0','leaf_1','lea..., dimensions={0} | all-to-all | bytes 524288 | tf_op jit(solution)/shard_map/all_to_all | solution.py:33
  355.2 11.9 %all_gather.26 = f32[128,64]{1,0:T(8,128)S(1)} all-gather(f32[32,64]{1,0:T(8,128)S(1)} %pad_maximum_fusion.5), channel_id=1, replica_groups=mesh['leaf_0'=8,'leaf_1'=4,'leaf_2'=2,'front'=4] {'front'}, dimensions={0}, use_global_device_ids=true | all-gather | bytes 40960 | tf_op jit(solution)/shard_map/all_gather | solution.py:44
  379.9 7.7 all_to_all.239
  389.1 18.6 %all_to_all.240 = f32[64,1,1024]{2,1,0:T(1,128)S(1)} all-to-all(f32[64,1,1024]{2,1,0:T(1,128)S(1)} %reshape.992), channel_id=1, replica_groups=mesh['leaf_0'=8,'leaf_1'=4,'leaf_2'=2,'front'=4] {'leaf_0','leaf_1','lea..., dimensions={0} | all-to-all | bytes 524288 | tf_op jit(solution)/shard_map/all_to_all | solution.py:33
  409.3 11.9 %all_gather.27 = f32[128,64]{1,0:T(8,128)S(1)} all-gather(f32[32,64]{1,0:T(8,128)S(1)} %concatenate.27), channel_id=1, replica_groups=mesh['leaf_0'=8,'leaf_1'=4,'leaf_2'=2,'front'=4] {'front'}, dimensions={0}, use_global_device_ids=true | all-gather | bytes 40960 | tf_op jit(solution)/shard_map/all_gather | solution.py:44
  434.7 7.0 all-to-all-start.24
  441.8 28.9 %all-to-all-done.24 = f32[64,1,32,128]{3,2,1,0:T(8,128)S(1)} async-done(((f32[64,1,32,128]{3,2,1,0:T(8,128)}), f32[64,1,32,128]{3,2,1,0:T(8,128)S(1)}, u32[]{:S(2)}, u32[]{:S(2)}) %all-to-all-start.24) | async-done | bytes 1048608 | tf_op jit(solution)/shard_map/all_to_all | solution.py:33
  492.0 6.2 all-to-all-start.27
  498.2 28.7 %all-to-all-done.27 = f32[64,1,32,128]{3,2,1,0:T(8,128)S(1)} async-done(((f32[64,1,32,128]{3,2,1,0:T(8,128)}), f32[64,1,32,128]{3,2,1,0:T(8,128)S(1)}, u32[]{:S(2)}, u32[]{:S(2)}) %all-to-all-start.27) | async-done | bytes 1048608 | tf_op jit(solution)/shard_map/all_to_all | solution.py:33
  527.0 8.0 all_to_all.241
  546.7 6.3 all-to-all-start.30
  553.0 28.8 %all-to-all-done.30 = f32[64,1,32,128]{3,2,1,0:T(8,128)S(1)} async-done(((f32[64,1,32,128]{3,2,1,0:T(8,128)}), f32[64,1,32,128]{3,2,1,0:T(8,128)S(1)}, u32[]{:S(2)}, u32[]{:S(2)}) %all-to-all-start.30) | async-done | bytes 1048608 | tf_op jit(solution)/shard_map/all_to_all | solution.py:33
  581.7 8.0 all_to_all.242
  601.4 6.8 all-to-all-start.33
  608.3 28.8 %all-to-all-done.33 = f32[64,1,32,128]{3,2,1,0:T(8,128)S(1)} async-done(((f32[64,1,32,128]{3,2,1,0:T(8,128)}), f32[64,1,32,128]{3,2,1,0:T(8,128)S(1)}, u32[]{:S(2)}, u32[]{:S(2)}) %all-to-all-start.33) | async-done | bytes 1048608 | tf_op jit(solution)/shard_map/all_to_all | solution.py:33
  637.0 8.0 all_to_all.243
  656.7 7.2 all-to-all-start.36
  663.9 28.8 %all-to-all-done.36 = f32[64,1,32,128]{3,2,1,0:T(8,128)S(1)} async-done(((f32[64,1,32,128]{3,2,1,0:T(8,128)}), f32[64,1,32,128]{3,2,1,0:T(8,128)S(1)}, u32[]{:S(2)}, u32[]{:S(2)}) %all-to-all-start.36) | async-done | bytes 1048608 | tf_op jit(solution)/shard_map/all_to_all | solution.py:33
  692.7 8.0 all_to_all.244
  719.8 28.8 %all-to-all-done.39 = f32[64,1,32,128]{3,2,1,0:T(8,128)S(1)} async-done(((f32[64,1,32,128]{3,2,1,0:T(8,128)}), f32[64,1,32,128]{3,2,1,0:T(8,128)S(1)}, u32[]{:S(2)}, u32[]{:S(2)}) %all-to-all-start.39) | async-done | bytes 1048608 | tf_op jit(solution)/shard_map/all_to_all | solution.py:33
  748.6 8.0 all_to_all.245
  774.3 28.5 %all-to-all-done.42 = f32[64,1,32,128]{3,2,1,0:T(8,128)S(1)} async-done(((f32[64,1,32,128]{3,2,1,0:T(8,128)}), f32[64,1,32,128]{3,2,1,0:T(8,128)S(1)}, u32[]{:S(2)}, u32[]{:S(2)}) %all-to-all-start.42) | async-done | bytes 1048608 | tf_op jit(solution)/shard_map/all_to_all | solution.py:33
  827.9 27.5 %psum.112 = f32[50,32]{0,1:T(8,128)S(1)} all-reduce(f32[50,32]{0,1:T(8,128)S(1)} %fusion.2), channel_id=1, replica_groups=mesh['leaf_0'=8,'leaf_1'=4,'leaf_2'=2,'front'=4] {'leaf_0'}, use_global_device_ids=true, to_apply=%region_47.48 | all-reduce | flops 1600 | bytes 12800 | tf_op jit(solution)/shard_map/psum | solution.py:55
  855.5 14.0 %psum.113 = f32[50,32]{0,1:T(8,128)S(1)} all-reduce(f32[50,32]{0,1:T(8,128)S(1)} %psum.112), channel_id=1, replica_groups=mesh['leaf_0'=8,'leaf_1'=4,'leaf_2'=2,'front'=4] {'leaf_1'}, use_global_device_ids=true, to_apply=%region_48.49 | all-reduce | flops 1600 | bytes 12800 | tf_op jit(solution)/shard_map/psum | solution.py:55
  872.8 15.3 %psum.115 = f32[50,32]{0,1:T(8,128)S(1)} all-reduce(f32[50,32]{0,1:T(8,128)S(1)} %psum.114), channel_id=1, replica_groups=mesh['leaf_0'=8,'leaf_1'=4,'leaf_2'=2,'front'=4] {'front'}, use_global_device_ids=true, to_apply=%region_50.51 | all-reduce | flops 1600 | bytes 12800 | tf_op jit(solution)/shard_map/psum | solution.py:55
  889.1 27.6 %all-reduce.1 = (f32[50,32]{0,1:T(8,128)S(1)}, f32[32,32]{0,1:T(8,128)S(1)}, f32[50,50]{1,0:T(8,128)S(1)}) all-reduce(f32[50,32]{0,1:T(8,128)S(1)} %fusion.1, f32[32,32]{0,1:T(8,128)S(1)} %convolution_add_fusion.3, f32[50,50]{1,0:T(8,128)S(1)} %convolution_add_fusion), channel_id=1, replica_groups=mesh['leaf_0'=8,'leaf_1'=4,'leaf_2'=2,'front'=4] {'leaf_0'}, use_global_device_ids=true, to_apply=%region_55.56 | all-reduce | flops 5124 | bytes 40992 | tf_op jit(solution)/shard_map/psum | solution.py:55
  916.6 17.1 %all-reduce.3 = (f32[50,32]{0,1:T(8,128)S(1)}, f32[32,32]{0,1:T(8,128)S(1)}, f32[50,50]{1,0:T(8,128)S(1)}) all-reduce(f32[50,32]{0,1:T(8,128)S(1)} %get-tuple-element.267, f32[32,32]{0,1:T(8,128)S(1)} %get-tuple-element.268, f32[50,50]{1,0:T(8,128)S(1)} %get-tuple-element.269), channel_id=1, replica_groups=mesh['leaf_0'=8,'leaf_1'=4,'leaf_2'=2,'front'=4] {'leaf_1'}, use_global_device_ids=true, to_apply=%region_56.57 | all-reduce | flops 5124 | bytes 40992 | tf_op jit(solution)/shard_map/psum | solution.py:55
  937.4 15.1 %all-reduce.2 = (f32[50,32]{0,1:T(8,128)S(1)}, f32[32,32]{0,1:T(8,128)S(1)}, f32[50,50]{1,0:T(8,128)S(1)}) all-reduce(f32[50,32]{0,1:T(8,128)S(1)} %get-tuple-element.276, f32[32,32]{0,1:T(8,128)S(1)} %get-tuple-element.277, f32[50,50]{1,0:T(8,128)S(1)} %get-tuple-element.278), channel_id=1, replica_groups=mesh['leaf_0'=8,'leaf_1'=4,'leaf_2'=2,'front'=4] {'front'}, use_global_device_ids=true, to_apply=%region_58.59 | all-reduce | flops 5124 | bytes 40992 | tf_op jit(solution)/shard_map/psum | solution.py:55
  (337 shorter events, 294.1 us)
Async XLA Ops:
  0.6 14.9 %copy-start = (f32[1,256,1024]{2,1,0:T(8,128)S(1)}, f32[1,256,1024]{2,1,0:T(8,128)}, u32[]{:S(2)}) copy-start(f32[1,256,1024]{2,1,0:T(8,128)} %param.42) | copy-start | bytes 3145732
  2.1 4.4 copy-start.10
  2.1 10.4 %all-to-all-start = ((f32[4,32,256]{2,1,0:T(8,128)}), f32[4,32,256]{2,1,0:T(8,128)S(1)}, u32[]{:S(2)}, u32[]{:S(2)}) async-start(f32[4,32,256]{2,1,0:T(8,128)} %broadcast_in_dim.197), calls=%async_computation | async-start | bytes 262144 | tf_op jit(solution)/shard_map/all_to_all | solution.py:33
  15.6 1.0 copy-start.8
  24.8 0.7 copy-start.12
  26.1 20.7 %all-to-all-start.2 = ((s32[64,1,128]{2,1,0:T(1,128)}), s32[64,1,128]{2,1,0:T(1,128)S(1)}, u32[]{:S(2)}, u32[]{:S(2)}) async-start(s32[64,1,128]{2,1,0:T(1,128)} %broadcast_in_dim.199), calls=%async_computation.2 | async-start | bytes 65536 | tf_op jit(solution)/shard_map/all_to_all | solution.py:33
  46.7 17.8 %all-to-all-start.4 = ((f32[64,1,1024]{2,1,0:T(1,128)}), f32[64,1,1024]{2,1,0:T(1,128)S(1)}, u32[]{:S(2)}, u32[]{:S(2)}) async-start(f32[64,1,1024]{2,1,0:T(1,128)} %reshape.968), calls=%async_computation.4 | async-start | bytes 524288 | tf_op jit(solution)/shard_map/all_to_all | solution.py:33
  80.7 0.7 copy-start.6
  80.7 10.2 %copy-start.1 = (f32[1,128,512]{2,1,0:T(8,128)S(1)}, f32[1,128,512]{2,1,0:T(8,128)}, u32[]{:S(2)}) copy-start(f32[1,128,512]{2,1,0:T(8,128)} %param.43) | copy-start | bytes 786436
  82.0 8.9 all-to-all-start.5
  90.9 0.7 copy-start.7
  91.6 0.8 copy-start.2
  100.7 0.7 copy-start.11
  101.9 14.2 %all-to-all-start.1 = ((s32[64,1,128]{2,1,0:T(1,128)}), s32[64,1,128]{2,1,0:T(1,128)S(1)}, u32[]{:S(2)}, u32[]{:S(2)}) async-start(s32[64,1,128]{2,1,0:T(1,128)} %broadcast_in_dim.198), calls=%async_computation.1 | async-start | bytes 65536 | tf_op jit(solution)/shard_map/all_to_all | solution.py:33
  116.2 17.8 %all-to-all-start.7 = ((f32[64,1,1024]{2,1,0:T(1,128)}), f32[64,1,1024]{2,1,0:T(1,128)S(1)}, u32[]{:S(2)}, u32[]{:S(2)}) async-start(f32[64,1,1024]{2,1,0:T(1,128)} %reshape.972), calls=%async_computation.7 | async-start | bytes 524288 | tf_op jit(solution)/shard_map/all_to_all | solution.py:33
  151.0 8.9 all-to-all-start.8
  205.9 8.9 all-to-all-start.11
  261.0 8.9 all-to-all-start.14
  280.6 18.8 %all-to-all-start.16 = ((f32[64,1,1024]{2,1,0:T(1,128)}), f32[64,1,1024]{2,1,0:T(1,128)S(1)}, u32[]{:S(2)}, u32[]{:S(2)}) async-start(f32[64,1,1024]{2,1,0:T(1,128)} %reshape.984), calls=%async_computation.16 | async-start | bytes 524288 | tf_op jit(solution)/shard_map/all_to_all | solution.py:33
  316.5 8.9 all-to-all-start.17
  370.5 8.9 all-to-all-start.20
  424.7 8.9 all-to-all-start.23
  434.7 35.9 %all-to-all-start.24 = ((f32[64,1,32,128]{3,2,1,0:T(8,128)}), f32[64,1,32,128]{3,2,1,0:T(8,128)S(1)}, u32[]{:S(2)}, u32[]{:S(2)}) async-start(f32[64,1,32,128]{3,2,1,0:T(8,128)} %broadcast_in_dim.214), calls=%async_computation.24 | async-start | bytes 2097152 | tf_op jit(solution)/shard_map/all_to_all | solution.py:33
  471.2 8.9 all-to-all-start.25
  480.3 0.8 copy-start.3
  482.0 8.9 all-to-all-start.26
  492.0 35.0 %all-to-all-start.27 = ((f32[64,1,32,128]{3,2,1,0:T(8,128)}), f32[64,1,32,128]{3,2,1,0:T(8,128)S(1)}, u32[]{:S(2)}, u32[]{:S(2)}) async-start(f32[64,1,32,128]{3,2,1,0:T(8,128)} %broadcast_in_dim.217), calls=%async_computation.27 | async-start | bytes 2097152 | tf_op jit(solution)/shard_map/all_to_all | solution.py:33
  536.7 8.9 all-to-all-start.29
  546.7 35.0 %all-to-all-start.30 = ((f32[64,1,32,128]{3,2,1,0:T(8,128)}), f32[64,1,32,128]{3,2,1,0:T(8,128)S(1)}, u32[]{:S(2)}, u32[]{:S(2)}) async-start(f32[64,1,32,128]{3,2,1,0:T(8,128)} %broadcast_in_dim.220), calls=%async_computation.30 | async-start | bytes 2097152 | tf_op jit(solution)/shard_map/all_to_all | solution.py:33
  591.4 8.9 all-to-all-start.32
  601.4 35.6 %all-to-all-start.33 = ((f32[64,1,32,128]{3,2,1,0:T(8,128)}), f32[64,1,32,128]{3,2,1,0:T(8,128)S(1)}, u32[]{:S(2)}, u32[]{:S(2)}) async-start(f32[64,1,32,128]{3,2,1,0:T(8,128)} %broadcast_in_dim.223), calls=%async_computation.33 | async-start | bytes 2097152 | tf_op jit(solution)/shard_map/all_to_all | solution.py:33
  646.7 8.9 all-to-all-start.35
  656.7 36.0 %all-to-all-start.36 = ((f32[64,1,32,128]{3,2,1,0:T(8,128)}), f32[64,1,32,128]{3,2,1,0:T(8,128)S(1)}, u32[]{:S(2)}, u32[]{:S(2)}) async-start(f32[64,1,32,128]{3,2,1,0:T(8,128)} %broadcast_in_dim.226), calls=%async_computation.36 | async-start | bytes 2097152 | tf_op jit(solution)/shard_map/all_to_all | solution.py:33
  702.3 8.9 all-to-all-start.38
  714.1 34.4 %all-to-all-start.39 = ((f32[64,1,32,128]{3,2,1,0:T(8,128)}), f32[64,1,32,128]{3,2,1,0:T(8,128)S(1)}, u32[]{:S(2)}, u32[]{:S(2)}) async-start(f32[64,1,32,128]{3,2,1,0:T(8,128)} %broadcast_in_dim.229), calls=%async_computation.39 | async-start | bytes 2097152 | tf_op jit(solution)/shard_map/all_to_all | solution.py:33
  758.2 8.9 all-to-all-start.41
  768.2 5.8 copy-start.4
  768.2 34.6 %all-to-all-start.42 = ((f32[64,1,32,128]{3,2,1,0:T(8,128)}), f32[64,1,32,128]{3,2,1,0:T(8,128)S(1)}, u32[]{:S(2)}, u32[]{:S(2)}) async-start(f32[64,1,32,128]{3,2,1,0:T(8,128)} %broadcast_in_dim.232), calls=%async_computation.42 | async-start | bytes 2097152 | tf_op jit(solution)/shard_map/all_to_all | solution.py:33
  803.5 8.9 all-to-all-start.43
  812.3 5.3 copy-start.5
  812.5 0.9 copy-start.9
  814.3 9.3 all-to-all-start.44
where the time goes:
time: 976 us; the launch traced here: 963 us
  blocking collectives  375 us (38%)
  waiting for transfers between devices  345 us (35%)
  starting transfers between devices  137 us (14%)
  local copies, waits for them, and re-layouts  50.8 us (5%)
  other arithmetic  40.4 us (4%)
  matrix products  11.6 us (1%)
    all_to_all x29, waiting for transfers between devices, from_everyone(): return lax.all_to_all(copies, axis, split_axis=0, concat_axis=0, tiled=True)  345 us
    all_to_all x29, starting transfers between devices, from_everyone(): return lax.all_to_all(copies, axis, split_axis=0, concat_axis=0, tiled=True)  137 us
    psum x8, blocking collectives, by_axis(): return functools.reduce(lax.psum, axes, array)  123 us
    all_to_all x9, blocking collectives, from_everyone(): return lax.all_to_all(copies, axis, split_axis=0, concat_axis=0, tiled=True)  114 us
    all_gather x7, blocking collectives, rows_first(): whole = lax.all_gather(both, axis, axis=0, tiled=True)  83.2 us
    all_to_all x7, blocking collectives, sum_at_owner(): lax.all_to_all(pieces, axis, split_axis=0, concat_axis=0, tiled=True)  54 us
    broadcast_in_dim x31, local copies, waits for them, and re-layouts, from_everyone(): copies = jnp.broadcast_to(array, (lax.axis_size(axis), *array.shape))  21 us
  transfers between devices with their start and end apart: 29, of which 29 were waited for; matrix products, arithmetic and copies ran while one was open for 1% of the time, Pallas kernels for 0%

commit v1 on v0

--- a/solution.py
+++ b/solution.py
@@ -41,7 +41,8 @@
     turned = [jnp.moveaxis(a, dim, 0) for a, dim in zip(arrays, dims)]
     widths = [t[0].size for t in turned]
     both = jnp.concatenate([t.reshape(-1, w) for t, w in zip(turned, widths)], axis=1)
-    whole = lax.all_gather(both, axis, axis=0, tiled=True)
+    sent = jnp.stack([both] * lax.axis_size(axis))
+    whole = jnp.concatenate(lax.all_to_all(sent, axis, 0, 0), axis=0)
     pieces = jnp.split(whole, [sum(widths[:k]) for k in range(1, len(widths))], axis=1)
     return tuple(
         (

time: 976 us -> 957 us (0.981)
  blocking collectives: 375 us -> 322 us
  waiting for transfers between devices: 345 us -> 361 us
  starting transfers between devices: 137 us -> 148 us
    all_gather x7 -> x0, blocking collectives: 83.2 us -> none  [rows_first(): whole = lax.all_gather(both, axis, axis=0, tiled=True)]
    all_to_all x0 -> x4, blocking collectives: none -> 31.6 us  [rows_first(): whole = jnp.concatenate(lax.all_to_all(sent, axis, 0, 0), axis=0)]
    all_to_all x0 -> x3, waiting for transfers between devices: none -> 16.2 us  [rows_first(): whole = jnp.concatenate(lax.all_to_all(sent, axis, 0, 0), axis=0)]
    all_to_all x0 -> x3, starting transfers between devices: none -> 9.79 us  [rows_first(): whole = jnp.concatenate(lax.all_to_all(sent, axis, 0, 0), axis=0)]
  transfers between devices with their start and end apart: 29 -> 32, of which waited for: 29 -> 32; matrix products, arithmetic and copies ran while one was open for 1% -> 1% of each run, Pallas kernels for 0% -> 0%
where the time goes in v1:
time: 957 us; the launch traced here: 945 us
  waiting for transfers between devices  361 us (38%)
  blocking collectives  322 us (34%)
  starting transfers between devices  148 us (15%)
  local copies, waits for them, and re-layouts  52.8 us (6%)
  other arithmetic  45.6 us (5%)
  matrix products  11.6 us (1%)
    all_to_all x29, waiting for transfers between devices, from_everyone(): return lax.all_to_all(copies, axis, split_axis=0, concat_axis=0, tiled=True)  345 us
    all_to_all x29, starting transfers between devices, from_everyone(): return lax.all_to_all(copies, axis, split_axis=0, concat_axis=0, tiled=True)  138 us
    psum x8, blocking collectives, by_axis(): return functools.reduce(lax.psum, axes, array)  124 us
    all_to_all x9, blocking collectives, from_everyone(): return lax.all_to_all(copies, axis, split_axis=0, concat_axis=0, tiled=True)  113 us
    all_to_all x7, blocking collectives, sum_at_owner(): lax.all_to_all(pieces, axis, split_axis=0, concat_axis=0, tiled=True)  54 us
    all_to_all x4, blocking collectives, rows_first(): whole = jnp.concatenate(lax.all_to_all(sent, axis, 0, 0), axis=0)  31.6 us
    broadcast_in_dim x31, local copies, waits for them, and re-layouts, from_everyone(): copies = jnp.broadcast_to(array, (lax.axis_size(axis), *array.shape))  21 us
  transfers between devices with their start and end apart: 32, of which 32 were waited for; matrix products, arithmetic and copies ran while one was open for 1% of the time, Pallas kernels for 0%

profile of v1, /device:TPU:8, one launch (start us, length us, event | category | flops | bytes accessed | tf_op | source)
XLA Modules:
  0.0 944.7 jit_solution(15925521521169875260)
XLA Ops:
  6.6 6.0 all-to-all-done
  17.1 7.7 all_to_all.265
  27.5 12.1 %all-to-all-start.4 = ((f32[64,1,1024]{2,1,0:T(1,128)}), f32[64,1,1024]{2,1,0:T(1,128)S(1)}, u32[]{:S(2)}, u32[]{:S(2)}) async-start(f32[64,1,1024]{2,1,0:T(1,128)} %reshape.1010), calls=%async_computation.4 | async-start | bytes 524288 | tf_op jit(solution)/shard_map/all_to_all | solution.py:33
  39.6 12.2 %all-to-all-done.4 = f32[64,1,1024]{2,1,0:T(1,128)S(1)} async-done(((f32[64,1,1024]{2,1,0:T(1,128)}), f32[64,1,1024]{2,1,0:T(1,128)S(1)}, u32[]{:S(2)}, u32[]{:S(2)}) %all-to-all-start.4) | async-done | bytes 262176 | tf_op jit(solution)/shard_map/all_to_all | solution.py:33
  60.5 6.1 all-to-all-done.2
  90.9 7.7 all_to_all.266
  106.6 12.3 %all-to-all-done.8 = f32[64,1,1024]{2,1,0:T(1,128)S(1)} async-done(((f32[64,1,1024]{2,1,0:T(1,128)}), f32[64,1,1024]{2,1,0:T(1,128)S(1)}, u32[]{:S(2)}, u32[]{:S(2)}) %all-to-all-start.8) | async-done | bytes 262176 | tf_op jit(solution)/shard_map/all_to_all | solution.py:33
  119.5 6.0 all-to-all-start.1
  127.9 6.1 all-to-all-done.1
  158.0 7.7 all_to_all.267
  167.1 16.7 %all_to_all.268 = f32[64,1,1024]{2,1,0:T(1,128)S(1)} all-to-all(f32[64,1,1024]{2,1,0:T(1,128)S(1)} %reshape.1022), channel_id=1, replica_groups=mesh['leaf_0'=8,'leaf_1'=4,'leaf_2'=2,'front'=4] {'leaf_0','leaf_1','lea..., dimensions={0} | all-to-all | bytes 524288 | tf_op jit(solution)/shard_map/all_to_all | solution.py:33
  185.7 7.8 all_to_all.269
  207.0 7.7 all_to_all.270
  216.2 19.4 %all_to_all.271 = f32[64,1,1024]{2,1,0:T(1,128)S(1)} all-to-all(f32[64,1,1024]{2,1,0:T(1,128)S(1)} %reshape.1028), channel_id=1, replica_groups=mesh['leaf_0'=8,'leaf_1'=4,'leaf_2'=2,'front'=4] {'leaf_0','leaf_1','lea..., dimensions={0} | all-to-all | bytes 524288 | tf_op jit(solution)/shard_map/all_to_all | solution.py:33
  237.4 8.2 all_to_all.272
  259.3 7.7 all_to_all.273
  269.2 6.6 all-to-all-start.20
  275.8 12.2 %all-to-all-done.20 = f32[64,1,1024]{2,1,0:T(1,128)S(1)} async-done(((f32[64,1,1024]{2,1,0:T(1,128)}), f32[64,1,1024]{2,1,0:T(1,128)S(1)}, u32[]{:S(2)}, u32[]{:S(2)}) %all-to-all-start.20) | async-done | bytes 262176 | tf_op jit(solution)/shard_map/all_to_all | solution.py:33
  312.9 7.7 all_to_all.274
  322.0 18.4 %all_to_all.275 = f32[64,1,1024]{2,1,0:T(1,128)S(1)} all-to-all(f32[64,1,1024]{2,1,0:T(1,128)S(1)} %reshape.1040), channel_id=1, replica_groups=mesh['leaf_0'=8,'leaf_1'=4,'leaf_2'=2,'front'=4] {'leaf_0','leaf_1','lea..., dimensions={0} | all-to-all | bytes 524288 | tf_op jit(solution)/shard_map/all_to_all | solution.py:33
  342.3 7.8 all_to_all.276
  364.0 7.7 all_to_all.277
  373.2 18.4 %all_to_all.278 = f32[64,1,1024]{2,1,0:T(1,128)S(1)} all-to-all(f32[64,1,1024]{2,1,0:T(1,128)S(1)} %reshape.1046), channel_id=1, replica_groups=mesh['leaf_0'=8,'leaf_1'=4,'leaf_2'=2,'front'=4] {'leaf_0','leaf_1','lea..., dimensions={0} | all-to-all | bytes 524288 | tf_op jit(solution)/shard_map/all_to_all | solution.py:33
  393.3 7.8 all_to_all.279
  415.5 7.0 all-to-all-start.31
  422.5 28.9 %all-to-all-done.31 = f32[64,1,32,128]{3,2,1,0:T(8,128)S(1)} async-done(((f32[64,1,32,128]{3,2,1,0:T(8,128)}), f32[64,1,32,128]{3,2,1,0:T(8,128)S(1)}, u32[]{:S(2)}, u32[]{:S(2)}) %all-to-all-start.31) | async-done | bytes 1048608 | tf_op jit(solution)/shard_map/all_to_all | solution.py:33
  472.8 6.2 all-to-all-start.34
  479.0 28.7 %all-to-all-done.34 = f32[64,1,32,128]{3,2,1,0:T(8,128)S(1)} async-done(((f32[64,1,32,128]{3,2,1,0:T(8,128)}), f32[64,1,32,128]{3,2,1,0:T(8,128)S(1)}, u32[]{:S(2)}, u32[]{:S(2)}) %all-to-all-start.34) | async-done | bytes 1048608 | tf_op jit(solution)/shard_map/all_to_all | solution.py:33
  507.8 8.0 all_to_all.280
  527.4 6.6 all-to-all-start.37
  534.0 28.6 %all-to-all-done.37 = f32[64,1,32,128]{3,2,1,0:T(8,128)S(1)} async-done(((f32[64,1,32,128]{3,2,1,0:T(8,128)}), f32[64,1,32,128]{3,2,1,0:T(8,128)S(1)}, u32[]{:S(2)}, u32[]{:S(2)}) %all-to-all-start.37) | async-done | bytes 1048608 | tf_op jit(solution)/shard_map/all_to_all | solution.py:33
  562.7 8.0 all_to_all.281
  582.3 6.9 all-to-all-start.40
  589.2 28.8 %all-to-all-done.40 = f32[64,1,32,128]{3,2,1,0:T(8,128)S(1)} async-done(((f32[64,1,32,128]{3,2,1,0:T(8,128)}), f32[64,1,32,128]{3,2,1,0:T(8,128)S(1)}, u32[]{:S(2)}, u32[]{:S(2)}) %all-to-all-start.40) | async-done | bytes 1048608 | tf_op jit(solution)/shard_map/all_to_all | solution.py:33
  618.0 8.0 all_to_all.282
  637.7 7.2 all-to-all-start.43
  644.9 28.8 %all-to-all-done.43 = f32[64,1,32,128]{3,2,1,0:T(8,128)S(1)} async-done(((f32[64,1,32,128]{3,2,1,0:T(8,128)}), f32[64,1,32,128]{3,2,1,0:T(8,128)S(1)}, u32[]{:S(2)}, u32[]{:S(2)}) %all-to-all-start.43) | async-done | bytes 1048608 | tf_op jit(solution)/shard_map/all_to_all | solution.py:33
  673.6 8.0 all_to_all.283
  700.8 28.8 %all-to-all-done.46 = f32[64,1,32,128]{3,2,1,0:T(8,128)S(1)} async-done(((f32[64,1,32,128]{3,2,1,0:T(8,128)}), f32[64,1,32,128]{3,2,1,0:T(8,128)S(1)}, u32[]{:S(2)}, u32[]{:S(2)}) %all-to-all-start.46) | async-done | bytes 1048608 | tf_op jit(solution)/shard_map/all_to_all | solution.py:33
  729.5 8.0 all_to_all.284
  749.2 5.8 all-to-all-start.49
  755.2 28.5 %all-to-all-done.49 = f32[64,1,32,128]{3,2,1,0:T(8,128)S(1)} async-done(((f32[64,1,32,128]{3,2,1,0:T(8,128)}), f32[64,1,32,128]{3,2,1,0:T(8,128)S(1)}, u32[]{:S(2)}, u32[]{:S(2)}) %all-to-all-start.49) | async-done | bytes 1048608 | tf_op jit(solution)/shard_map/all_to_all | solution.py:33
  808.9 27.5 %psum.112 = f32[50,32]{0,1:T(8,128)S(1)} all-reduce(f32[50,32]{0,1:T(8,128)S(1)} %fusion.2), channel_id=1, replica_groups=mesh['leaf_0'=8,'leaf_1'=4,'leaf_2'=2,'front'=4] {'leaf_0'}, use_global_device_ids=true, to_apply=%region_47.48 | all-reduce | flops 1600 | bytes 12800 | tf_op jit(solution)/shard_map/psum | solution.py:56
  836.4 14.0 %psum.113 = f32[50,32]{0,1:T(8,128)S(1)} all-reduce(f32[50,32]{0,1:T(8,128)S(1)} %psum.112), channel_id=1, replica_groups=mesh['leaf_0'=8,'leaf_1'=4,'leaf_2'=2,'front'=4] {'leaf_1'}, use_global_device_ids=true, to_apply=%region_48.49 | all-reduce | flops 1600 | bytes 12800 | tf_op jit(solution)/shard_map/psum | solution.py:56
  854.0 15.3 %psum.115 = f32[50,32]{0,1:T(8,128)S(1)} all-reduce(f32[50,32]{0,1:T(8,128)S(1)} %psum.114), channel_id=1, replica_groups=mesh['leaf_0'=8,'leaf_1'=4,'leaf_2'=2,'front'=4] {'front'}, use_global_device_ids=true, to_apply=%region_50.51 | all-reduce | flops 1600 | bytes 12800 | tf_op jit(solution)/shard_map/psum | solution.py:56
  870.3 27.6 %all-reduce.1 = (f32[50,32]{0,1:T(8,128)S(1)}, f32[32,32]{0,1:T(8,128)S(1)}, f32[50,50]{1,0:T(8,128)S(1)}) all-reduce(f32[50,32]{0,1:T(8,128)S(1)} %fusion.1, f32[32,32]{0,1:T(8,128)S(1)} %convolution_add_fusion.3, f32[50,50]{1,0:T(8,128)S(1)} %convolution_add_fusion), channel_id=1, replica_groups=mesh['leaf_0'=8,'leaf_1'=4,'leaf_2'=2,'front'=4] {'leaf_0'}, use_global_device_ids=true, to_apply=%region_55.56 | all-reduce | flops 5124 | bytes 40992 | tf_op jit(solution)/shard_map/psum | solution.py:56
  897.9 17.1 %all-reduce.3 = (f32[50,32]{0,1:T(8,128)S(1)}, f32[32,32]{0,1:T(8,128)S(1)}, f32[50,50]{1,0:T(8,128)S(1)}) all-reduce(f32[50,32]{0,1:T(8,128)S(1)} %get-tuple-element.267, f32[32,32]{0,1:T(8,128)S(1)} %get-tuple-element.268, f32[50,50]{1,0:T(8,128)S(1)} %get-tuple-element.269), channel_id=1, replica_groups=mesh['leaf_0'=8,'leaf_1'=4,'leaf_2'=2,'front'=4] {'leaf_1'}, use_global_device_ids=true, to_apply=%region_56.57 | all-reduce | flops 5124 | bytes 40992 | tf_op jit(solution)/shard_map/psum | solution.py:56
  918.6 15.1 %all-reduce.2 = (f32[50,32]{0,1:T(8,128)S(1)}, f32[32,32]{0,1:T(8,128)S(1)}, f32[50,50]{1,0:T(8,128)S(1)}) all-reduce(f32[50,32]{0,1:T(8,128)S(1)} %get-tuple-element.276, f32[32,32]{0,1:T(8,128)S(1)} %get-tuple-element.277, f32[50,50]{1,0:T(8,128)S(1)} %get-tuple-element.278), channel_id=1, replica_groups=mesh['leaf_0'=8,'leaf_1'=4,'leaf_2'=2,'front'=4] {'front'}, use_global_device_ids=true, to_apply=%region_58.59 | all-reduce | flops 5124 | bytes 40992 | tf_op jit(solution)/shard_map/psum | solution.py:56
  (368 shorter events, 310.2 us)
Async XLA Ops:
  0.6 14.9 %copy-start = (f32[1,256,1024]{2,1,0:T(8,128)S(1)}, f32[1,256,1024]{2,1,0:T(8,128)}, u32[]{:S(2)}) copy-start(f32[1,256,1024]{2,1,0:T(8,128)} %param.42) | copy-start | bytes 3145732
  2.1 4.4 copy-start.10
  2.1 10.4 %all-to-all-start = ((f32[4,32,256]{2,1,0:T(8,128)}), f32[4,32,256]{2,1,0:T(8,128)S(1)}, u32[]{:S(2)}, u32[]{:S(2)}) async-start(f32[4,32,256]{2,1,0:T(8,128)} %broadcast_in_dim.197), calls=%async_computation | async-start | bytes 262144 | tf_op jit(solution)/shard_map/all_to_all | solution.py:33
  15.6 1.0 copy-start.8
  27.5 24.3 %all-to-all-start.4 = ((f32[64,1,1024]{2,1,0:T(1,128)}), f32[64,1,1024]{2,1,0:T(1,128)S(1)}, u32[]{:S(2)}, u32[]{:S(2)}) async-start(f32[64,1,1024]{2,1,0:T(1,128)} %reshape.1010), calls=%async_computation.4 | async-start | bytes 524288 | tf_op jit(solution)/shard_map/all_to_all | solution.py:33
  39.6 12.2 %copy-start.12 = (s32[1,128]{1,0:T(1,128)S(1)}, s32[1,128]{1,0:T(1,128)}, u32[]{:S(2)}) copy-start(s32[1,128]{1,0:T(1,128)} %param.48) | copy-start | bytes 1540
  52.4 14.2 %all-to-all-start.2 = ((s32[64,1,128]{2,1,0:T(1,128)}), s32[64,1,128]{2,1,0:T(1,128)S(1)}, u32[]{:S(2)}, u32[]{:S(2)}) async-start(s32[64,1,128]{2,1,0:T(1,128)} %broadcast_in_dim.199), calls=%async_computation.2 | async-start | bytes 65536 | tf_op jit(solution)/shard_map/all_to_all | solution.py:33
  66.6 8.7 all-to-all-start.5
  78.7 0.7 copy-start.6
  78.7 10.2 %copy-start.1 = (f32[1,128,512]{2,1,0:T(8,128)S(1)}, f32[1,128,512]{2,1,0:T(8,128)}, u32[]{:S(2)}) copy-start(f32[1,128,512]{2,1,0:T(8,128)} %param.43) | copy-start | bytes 786436
  80.0 8.9 all-to-all-start.6
  88.9 0.7 copy-start.7
  89.6 0.8 copy-start.2
  100.8 18.1 %all-to-all-start.8 = ((f32[64,1,1024]{2,1,0:T(1,128)}), f32[64,1,1024]{2,1,0:T(1,128)S(1)}, u32[]{:S(2)}, u32[]{:S(2)}) async-start(f32[64,1,1024]{2,1,0:T(1,128)} %reshape.1016), calls=%async_computation.8 | async-start | bytes 524288 | tf_op jit(solution)/shard_map/all_to_all | solution.py:33
  106.6 12.3 %copy-start.11 = (s32[1,128]{1,0:T(1,128)S(1)}, s32[1,128]{1,0:T(1,128)}, u32[]{:S(2)}) copy-start(s32[1,128]{1,0:T(1,128)} %param.49) | copy-start | bytes 1540
  119.5 14.5 %all-to-all-start.1 = ((s32[64,1,128]{2,1,0:T(1,128)}), s32[64,1,128]{2,1,0:T(1,128)S(1)}, u32[]{:S(2)}, u32[]{:S(2)}) async-start(s32[64,1,128]{2,1,0:T(1,128)} %broadcast_in_dim.198), calls=%async_computation.1 | async-start | bytes 65536 | tf_op jit(solution)/shard_map/all_to_all | solution.py:33
  134.0 8.7 all-to-all-start.9
  146.8 8.9 all-to-all-start.10
  197.6 8.9 all-to-all-start.14
  249.9 8.9 all-to-all-start.18
  269.2 18.8 %all-to-all-start.20 = ((f32[64,1,1024]{2,1,0:T(1,128)}), f32[64,1,1024]{2,1,0:T(1,128)S(1)}, u32[]{:S(2)}, u32[]{:S(2)}) async-start(f32[64,1,1024]{2,1,0:T(1,128)} %reshape.1034), calls=%async_computation.20 | async-start | bytes 524288 | tf_op jit(solution)/shard_map/all_to_all | solution.py:33
  290.4 8.7 all-to-all-start.21
  303.4 8.9 all-to-all-start.22
  354.6 8.9 all-to-all-start.26
  405.5 8.9 all-to-all-start.30
  415.5 35.9 %all-to-all-start.31 = ((f32[64,1,32,128]{3,2,1,0:T(8,128)}), f32[64,1,32,128]{3,2,1,0:T(8,128)S(1)}, u32[]{:S(2)}, u32[]{:S(2)}) async-start(f32[64,1,32,128]{3,2,1,0:T(8,128)} %broadcast_in_dim.214), calls=%async_computation.31 | async-start | bytes 2097152 | tf_op jit(solution)/shard_map/all_to_all | solution.py:33
  452.0 8.9 all-to-all-start.32
  461.0 0.8 copy-start.3
  462.7 8.9 all-to-all-start.33
  472.8 35.0 %all-to-all-start.34 = ((f32[64,1,32,128]{3,2,1,0:T(8,128)}), f32[64,1,32,128]{3,2,1,0:T(8,128)S(1)}, u32[]{:S(2)}, u32[]{:S(2)}) async-start(f32[64,1,32,128]{3,2,1,0:T(8,128)} %broadcast_in_dim.217), calls=%async_computation.34 | async-start | bytes 2097152 | tf_op jit(solution)/shard_map/all_to_all | solution.py:33
  517.4 8.9 all-to-all-start.36
  527.4 35.2 %all-to-all-start.37 = ((f32[64,1,32,128]{3,2,1,0:T(8,128)}), f32[64,1,32,128]{3,2,1,0:T(8,128)S(1)}, u32[]{:S(2)}, u32[]{:S(2)}) async-start(f32[64,1,32,128]{3,2,1,0:T(8,128)} %broadcast_in_dim.220), calls=%async_computation.37 | async-start | bytes 2097152 | tf_op jit(solution)/shard_map/all_to_all | solution.py:33
  572.3 8.9 all-to-all-start.39
  582.3 35.6 %all-to-all-start.40 = ((f32[64,1,32,128]{3,2,1,0:T(8,128)}), f32[64,1,32,128]{3,2,1,0:T(8,128)S(1)}, u32[]{:S(2)}, u32[]{:S(2)}) async-start(f32[64,1,32,128]{3,2,1,0:T(8,128)} %broadcast_in_dim.223), calls=%async_computation.40 | async-start | bytes 2097152 | tf_op jit(solution)/shard_map/all_to_all | solution.py:33
  627.6 8.9 all-to-all-start.42
  637.7 36.0 %all-to-all-start.43 = ((f32[64,1,32,128]{3,2,1,0:T(8,128)}), f32[64,1,32,128]{3,2,1,0:T(8,128)S(1)}, u32[]{:S(2)}, u32[]{:S(2)}) async-start(f32[64,1,32,128]{3,2,1,0:T(8,128)} %broadcast_in_dim.226), calls=%async_computation.43 | async-start | bytes 2097152 | tf_op jit(solution)/shard_map/all_to_all | solution.py:33
  683.3 8.9 all-to-all-start.45
  695.1 34.4 %all-to-all-start.46 = ((f32[64,1,32,128]{3,2,1,0:T(8,128)}), f32[64,1,32,128]{3,2,1,0:T(8,128)S(1)}, u32[]{:S(2)}, u32[]{:S(2)}) async-start(f32[64,1,32,128]{3,2,1,0:T(8,128)} %broadcast_in_dim.229), calls=%async_computation.46 | async-start | bytes 2097152 | tf_op jit(solution)/shard_map/all_to_all | solution.py:33
  739.2 8.9 all-to-all-start.48
  749.2 5.8 copy-start.4
  749.2 34.6 %all-to-all-start.49 = ((f32[64,1,32,128]{3,2,1,0:T(8,128)}), f32[64,1,32,128]{3,2,1,0:T(8,128)S(1)}, u32[]{:S(2)}, u32[]{:S(2)}) async-start(f32[64,1,32,128]{3,2,1,0:T(8,128)} %broadcast_in_dim.232), calls=%async_computation.49 | async-start | bytes 2097152 | tf_op jit(solution)/shard_map/all_to_all | solution.py:33
  784.4 8.9 all-to-all-start.50
  793.3 5.3 copy-start.5
  793.4 0.9 copy-start.9
  795.3 9.3 all-to-all-start.51
